TPU v7x, 32 devices: a whole 2x2x4 slice. The times are simulated.
32 devices in a mesh: src: 8 (over z, core), cand: 4 (over y, x).
Axes of the slice: x: 2, y: 2, z: 4, core: 2. Of those that a mesh axis runs over, the one named last changes fastest.
Arguments:
- layer_input: bfloat16 [32, 128, 1024], P(('src', 'cand')), parts along dimension 0, may hold values from -16 to 16
- token_ids: int32 [32, 128], P(('src', 'cand')), parts along dimension 0, may hold values from 0 to 50264
- lengths: int32 [32], P(('src', 'cand')), parts along dimension 0, may hold values from 32 to 128
- idf_table: float32 [402120], P('src'), parts along dimension 0, may hold values from 1 to 12
- query_weight: bfloat16 [1024, 1024], P('cand'), may hold values from -0.1875 to 0.1875
- key_weight: bfloat16 [1024, 1024], P('cand'), may hold values from -0.1875 to 0.1875
- value_weight: bfloat16 [1024, 1024], P('cand'), may hold values from -0.1875 to 0.1875
- output_weight: bfloat16 [1024, 1024], P('cand'), may hold values from -0.1875 to 0.1875
Outputs:
- embedded: bfloat16 [32, 128, 1024], P(('src', 'cand')), parts along dimension 0
- pair_utility: float32 [32, 4], P(('src', 'cand')), parts along dimension 0
- expected_utility: float32 [32], P(('src', 'cand')), parts along dimension 0
There are 8 independent parts, one for each index of `src`. A program takes and returns all parts, laid end to end along the dimension named above; an argument that names none is the same for every part. Nothing has to cross between parts.
All inputs are finite; a program needn't handle non-finite values.
Results may differ from a plain program's by a relative error of at most 0.0086.
Values may be sent and summed in bfloat16 or wider, within the bound.
A program may use at most 64 MiB of HBM per device.

v0:
```python
import functools
import math

import jax
import jax.numpy as jnp
from jax import lax
from jax.experimental import pallas as pl
from jax.experimental.pallas import tpu as pltpu
from jax.sharding import PartitionSpec as P

HEAD = 64


def block_utility(own_vectors, own_weight, far_vectors, far_weight):
    own_count, length, width = own_vectors.shape
    far_count = far_vectors.shape[0]
    similar = lax.dot_general(
        own_vectors.reshape(own_count * length, width),
        far_vectors.reshape(far_count * length, width),
        (((1,), (1,)), ((), ())),
        preferred_element_type=jnp.float32,
    )
    similar = similar.reshape(own_count, length, far_count, length)
    own_usable = own_weight > 0
    far_usable = far_weight > 0
    best_far = jnp.max(jnp.where(far_usable[None, None, :, :], similar, -4.0), axis=3)
    best_own = jnp.max(jnp.where(own_usable[:, :, None, None], similar, -4.0), axis=1)
    own_float = own_weight.astype(jnp.float32)
    far_float = far_weight.astype(jnp.float32)
    forward = jnp.einsum("il,ilj->ij", own_float, best_far, precision=lax.Precision.HIGHEST)
    forward = forward / jnp.sum(own_float, axis=1)[:, None]
    backward = jnp.einsum("jm,ijm->ij", far_float, best_own, precision=lax.Precision.HIGHEST)
    backward = backward / jnp.sum(far_float, axis=1)[None, :]
    return 0.5 * (forward + backward)


def gathered_shards(
    layer_input,
    token_ids,
    lengths,
    idf_table,
    query_weight,
    key_weight,
    value_weight,
    output_weight,
):
    local_cands, length, width = layer_input.shape
    cycle_size = lax.axis_size("cand")
    all_cands = local_cands * cycle_size
    head_size = HEAD
    head_count = width // head_size
    flat = layer_input.reshape(local_cands * length, width)
    pieces = (
        lax.all_gather(query_weight, "cand", axis=0, tiled=True),
        lax.all_gather(key_weight, "cand", axis=0, tiled=True),
        lax.all_gather(value_weight, "cand", axis=0, tiled=True),
    )
    columns = flat
    queries, key_rows, value_rows = tuple(
        (jnp.dot(columns, piece, preferred_element_type=jnp.float32) for piece in pieces)
    )
    queries = queries.astype(jnp.bfloat16).reshape(local_cands, length, head_count, head_size)
    key_rows = key_rows.astype(jnp.bfloat16).reshape(local_cands, length, head_count, head_size)
    value_rows = value_rows.astype(jnp.bfloat16).reshape(local_cands, length, head_count, head_size)
    positions = jnp.arange(length, dtype=jnp.int32)
    valid = positions[None, :] < lengths[:, None]
    scale = 1.0 / math.sqrt(head_size)
    scores = (
        jnp.einsum("clhe,cmhe->chlm", queries, key_rows, preferred_element_type=jnp.float32) * scale
    )
    scores = jnp.where(valid[:, None, None, :], scores, -1000000000.0)
    highest = jnp.max(scores, axis=-1, keepdims=True)
    expo = jnp.exp(scores - highest)
    probs = (expo / jnp.sum(expo, axis=-1, keepdims=True)).astype(jnp.bfloat16)
    context = jnp.einsum("chlm,cmhe->clhe", probs, value_rows, preferred_element_type=jnp.float32)
    context = context.astype(jnp.bfloat16).reshape(local_cands * length, width)
    columns = context
    mixed = jnp.dot(
        columns,
        lax.all_gather(output_weight, "cand", axis=0, tiled=True),
        preferred_element_type=jnp.float32,
    ) + flat.astype(jnp.float32)
    centred = mixed - jnp.mean(mixed, axis=-1, keepdims=True)
    squares = jnp.sum(centred * centred, axis=-1, keepdims=True)
    embedded = (
        (centred / jnp.sqrt(squares + 0.001))
        .astype(jnp.bfloat16)
        .reshape(local_cands, length, width)
    )
    token_weight = (jnp.take(idf_table, token_ids, axis=0) * valid.astype(jnp.float32)).astype(
        jnp.bfloat16
    )
    myself = lax.axis_index("cand")
    piece = (
        lax.all_gather(embedded, "cand", axis=0, tiled=True),
        lax.all_gather(token_weight, "cand", axis=0, tiled=True),
    )
    utility = block_utility(embedded, token_weight, piece[0], piece[1])
    blocks = utility.reshape(local_cands, cycle_size, local_cands)
    own_part = lax.dynamic_slice(blocks, (0, myself, 0), (local_cands, 1, local_cands))[:, 0, :]
    diagonal = jnp.diagonal(own_part)
    expected_utility = (jnp.sum(utility, axis=1) - diagonal) / (all_cands - 1)
    return (embedded, utility, expected_utility)


def remote(src_ref, dst_ref, send_sem, recv_sem, device):
    return pltpu.make_async_remote_copy(
        src_ref=src_ref,
        dst_ref=dst_ref,
        send_sem=send_sem,
        recv_sem=recv_sem,
        device_id=device,
        device_id_type=pl.DeviceIdType.MESH,
    )


def flipped(index, bits):
    result = index
    place = 1
    while place <= bits:
        if bits & place:
            digit = lax.rem(lax.div(index, place), 2)
            result = result + place - 2 * place * digit
        place *= 2
    return result


def kernel(
    count,
    x_hbm,
    ids_hbm,
    used,
    table_hbm,
    q_hbm,
    k_hbm,
    v_hbm,
    o_hbm,
    embedded_ref,
    utility_ref,
    expected_ref,
    stage,
    full,
    out_full,
    x_all,
    meta,
    context_out,
    context_full,
    vectors,
    ids,
    table,
    local_sem,
    send_sem,
    recv_sem,
):
    group, me = lax.axis_index("src"), lax.axis_index("cand")
    share = lax.rem(group, 4)
    sibling = (flipped(group, 1), me)
    mate = (flipped(group, 2), me)
    others = range(1, count)
    peer = [(group, flipped(me, bits)) for bits in range(count)]
    length, width = x_hbm.shape
    rows, columns = stage.shape[1], full.shape[2]
    quarter, middle = rows // 4, length // 2
    started = []

    def push(src_ref, dst_ref, device):
        number = len(started)
        copy = remote(src_ref, dst_ref, send_sem.at[number], recv_sem.at[number], device)
        copy.start()
        started.append(copy)
        return copy

    def column_block(index):
        return pl.ds(pl.multiple_of(index * columns, columns), columns)

    def row_block(index):
        return pl.ds(pl.multiple_of(index * rows, rows), rows)

    def row_share(index, which):
        return pl.ds(pl.multiple_of(index * rows + which * quarter, quarter), quarter)

    own_share = pl.ds(pl.multiple_of(share * quarter, quarter), quarter)
    mate_share = lax.rem(share + 2, 4)

    weights = (q_hbm, k_hbm, v_hbm)
    loads = [pltpu.make_async_copy(w, stage.at[t], local_sem.at[t]) for t, w in enumerate(weights)]
    loads += [
        pltpu.make_async_copy(o_hbm, out_full.at[row_block(me), :], local_sem.at[3]),
        pltpu.make_async_copy(x_hbm, x_all.at[0], local_sem.at[4]),
        pltpu.make_async_copy(ids_hbm, ids, local_sem.at[5]),
    ]
    loads += [
        pltpu.make_async_copy(
            w.at[:, column_block(me)], full.at[t, row_block(me), :], local_sem.at[6 + t]
        )
        for t, w in enumerate(weights)
    ]
    loads += [
        pltpu.make_async_copy(table_hbm, table, local_sem.at[9]),
    ]
    for load in loads:
        load.start()

    barrier = pltpu.get_barrier_semaphore()
    targets = [sibling, mate] + [peer[r] for r in others]
    for target in targets:
        pl.semaphore_signal(barrier, inc=1, device_id=target, device_id_type=pl.DeviceIdType.MESH)
    pl.semaphore_wait(barrier, len(targets))

    def exchange(held):
        part = [held.at[0, pl.ds(0, middle), :], held.at[0, pl.ds(middle, middle), :]]

        def slot(r, which):
            return held.at[r, pl.ds(which * middle, middle), :]

        first = {1: push(part[0], slot(1, 0), peer[1]), 2: push(part[1], slot(2, 1), peer[2])}
        second = {1: push(part[1], slot(1, 1), peer[1]), 2: push(part[0], slot(2, 0), peer[2])}

        def relay():
            first[1].wait_recv()
            near = push(slot(1, 0), slot(3, 0), peer[2])
            first[2].wait_recv()
            return (near, push(slot(2, 1), slot(3, 1), peer[1]))

        return second, relay

    for t in range(3):
        loads[t].wait()
    w_copies = {}
    for r in others:
        w_copies[r] = push(
            stage.at[:, own_share, column_block(peer[r][1])],
            full.at[:, row_share(me, share), :],
            peer[r],
        )
    for load in loads[3:6]:
        load.wait()
    o_copies = {
        r: push(out_full.at[row_share(me, share), :], out_full.at[row_share(me, share), :], peer[r])
        for r in others
    }
    x_second, x_relay = exchange(x_all)
    for load in loads[6:]:
        load.wait()

    position = lax.broadcasted_iota(jnp.int32, (1, length), 1)

    def look_up(at, weights_row):
        return jnp.where(position == at, table[ids[0, at]], weights_row)

    valid_row = (position < used[0]).astype(jnp.float32)
    weights_row = lax.fori_loop(0, length, look_up, jnp.zeros((1, length), jnp.float32), unroll=8)
    weights_row = (weights_row * valid_row).astype(jnp.bfloat16).astype(jnp.float32)
    meta[0] = jnp.concatenate([weights_row, jnp.broadcast_to(valid_row, (7, length))], axis=0)
    m_copies = {r: push(meta.at[0], meta.at[r], peer[r]) for r in others}

    def spread(copy, landed):
        copy.wait_recv()
        return (push(landed, landed, mate), push(landed, landed, sibling))

    def hand_over(copy, landed):
        copy.wait_recv()
        return push(landed, landed, sibling)

    def full_share(r, which):
        return full.at[:, row_share(peer[r][1], which), :]

    def out_share(r, which):
        return out_full.at[row_share(peer[r][1], which), :]

    w_spread = {r: spread(w_copies[r], full_share(r, share)) for r in others}
    o_spread = {}
    o_hand = {}
    for r in others:
        o_spread[r] = spread(o_copies[r], out_share(r, share))
    w_hand = {r: hand_over(w_spread[r][0], full_share(r, mate_share)) for r in others}
    x_far = x_relay()
    for r in others:
        w_spread[r][1].wait_recv()
        w_hand[r].wait_recv()

    lane = lax.broadcasted_iota(jnp.int32, (1, 2 * HEAD), 1)
    scale = 1.0 / math.sqrt(HEAD)
    first = (lane < HEAD).astype(jnp.float32)
    keep = [(first * scale).astype(jnp.bfloat16), ((1.0 - first) * scale).astype(jnp.bfloat16)]

    def context_of(r):
        rows_in = x_all[r]
        queries, key_rows, value_rows = tuple(
            jnp.dot(rows_in, full[t], preferred_element_type=jnp.float32).astype(jnp.bfloat16)
            for t in range(3)
        )
        valid = meta[r, 1:2, :] > 0.0
        pieces = []
        for start in range(0, columns, 2 * HEAD):
            span = slice(start, start + 2 * HEAD)
            q_pair, k_pair, v_pair = queries[:, span], key_rows[:, span], value_rows[:, span]
            stacked = jnp.concatenate([q_pair * keep[0], q_pair * keep[1]], axis=0)
            scores = lax.dot_general(
                stacked, k_pair, (((1,), (1,)), ((), ())), preferred_element_type=jnp.float32
            )
            scores = jnp.where(valid, scores, -1000000000.0)
            expo = jnp.exp(scores - jnp.max(scores, axis=-1, keepdims=True))
            total = jnp.sum(expo, axis=-1, keepdims=True)
            summed = jnp.dot(
                expo.astype(jnp.bfloat16), v_pair, preferred_element_type=jnp.float32
            )
            summed = summed / total
            pieces.append(jnp.where(lane < HEAD, summed[:length], summed[length:]))
        return jnp.concatenate(pieces, axis=1).astype(jnp.bfloat16)

    context_full[:, column_block(me)] = context_of(0)
    c_copies = []
    for r in others:
        m_copies[r].wait_recv()
        for copy in ((x_second[r],) if r < 3 else x_far):
            copy.wait_recv()
        context_out[r] = context_of(r)
        c_copies.append(push(context_out.at[r], context_full.at[:, column_block(me)], peer[r]))
        if r == 2:
            for q in others:
                o_hand[q] = hand_over(o_spread[q][0], out_share(q, mate_share))
    for r in others:
        o_spread[r][1].wait_recv()
        o_hand[r].wait_recv()
    for copy in c_copies:
        copy.wait_recv()

    mixed = jnp.dot(context_full[...], out_full[...], preferred_element_type=jnp.float32)
    mixed = mixed + x_all[0].astype(jnp.float32)
    centred = mixed - jnp.mean(mixed, axis=-1, keepdims=True)
    squares = jnp.sum(centred * centred, axis=-1, keepdims=True)
    own = (centred / jnp.sqrt(squares + 0.001)).astype(jnp.bfloat16)
    vectors[0] = own
    e_second, e_relay = exchange(vectors)
    embedded_ref[...] = own

    own_weight = meta[0, 0:1, :]
    own_column = jnp.broadcast_to(own_weight, (length, length)).T
    own_total = jnp.sum(own_weight, axis=1, keepdims=True)
    slot = lax.broadcasted_iota(jnp.int32, utility_ref.shape, 1)

    def pair_of(r):
        far_weight = meta[r, 0:1, :]
        similar = lax.dot_general(
            own, vectors[r], (((1,), (1,)), ((), ())), preferred_element_type=jnp.float32
        )
        best_far = jnp.max(jnp.where(far_weight > 0, similar, -4.0), axis=1, keepdims=True)
        best_own = jnp.max(jnp.where(own_column > 0, similar, -4.0), axis=0, keepdims=True)
        forward = jnp.sum(own_column[:, 0:1] * best_far, axis=0, keepdims=True) / own_total
        backward = jnp.sum(far_weight * best_own, axis=1, keepdims=True) / jnp.sum(
            far_weight, axis=1, keepdims=True
        )
        return 0.5 * (forward + backward)

    diagonal = pair_of(0)
    e_far = e_relay()
    utility = jnp.where(slot == me, diagonal, 0.0)
    everything = diagonal
    for r in others:
        for copy in ((e_second[r],) if r < 3 else e_far):
            copy.wait_recv()
        pair = pair_of(r)
        utility = jnp.where(slot == peer[r][1], pair, utility)
        everything = everything + pair
    utility_ref[...] = utility
    expected_ref[...] = (everything - diagonal) / (count - 1)

    for copy in started:
        copy.wait_send()


def shards(
    sizes,
    layer_input,
    token_ids,
    lengths,
    idf_table,
    query_weight,
    key_weight,
    value_weight,
    output_weight,
):
    local_cands, length, width = layer_input.shape
    count = sizes["cand"]
    rows = query_weight.shape[0]
    columns = width // count
    if (
        local_cands != 1
        or count != 4
        or sizes["src"] % 4
        or columns % (2 * HEAD)
        or rows % 64
        or length != 128
    ):
        return gathered_shards(
            layer_input,
            token_ids,
            lengths,
            idf_table,
            query_weight,
            key_weight,
            value_weight,
            output_weight,
        )
    anywhere = pl.BlockSpec(memory_space=pl.ANY)
    in_vmem = pl.BlockSpec(memory_space=pltpu.VMEM)
    copies = pltpu.SemaphoreType.DMA((42,))
    embedded, utility, expected = pl.pallas_call(
        functools.partial(kernel, count),
        out_shape=(
            pltpu.VMEM((length, width), jnp.bfloat16),
            pltpu.VMEM((1, count), jnp.float32),
            pltpu.VMEM((1, 1), jnp.float32),
        ),
        in_specs=[anywhere] * 2 + [pl.BlockSpec(memory_space=pltpu.SMEM)] + [anywhere] * 5,
        out_specs=(in_vmem, in_vmem, in_vmem),
        scratch_shapes=[
            pltpu.VMEM((3, rows, width), jnp.bfloat16),
            pltpu.VMEM((3, rows * count, columns), jnp.bfloat16),
            pltpu.VMEM((rows * count, width), jnp.bfloat16),
            pltpu.VMEM((count, length, width), jnp.bfloat16),
            pltpu.VMEM((count, 8, length), jnp.float32),
            pltpu.VMEM((count, length, columns), jnp.bfloat16),
            pltpu.VMEM((length, width), jnp.bfloat16),
            pltpu.VMEM((count, length, width), jnp.bfloat16),
            pltpu.SMEM((1, length), jnp.int32),
            pltpu.SMEM(idf_table.shape, jnp.float32),
            pltpu.SemaphoreType.DMA((10,)),
            copies,
            copies,
        ],
        compiler_params=pltpu.CompilerParams(collective_id=0, has_side_effects=True),
    )(
        layer_input.reshape(length, width),
        token_ids,
        lengths,
        idf_table,
        query_weight,
        key_weight,
        value_weight,
        output_weight,
    )
    return (embedded.reshape(1, length, width), utility, expected.reshape(1))


def solution(mesh):
    in_specs = (
        P(("src", "cand"), None, None),
        P(("src", "cand"), None),
        P(("src", "cand")),
        P("src"),
        P("cand", None),
        P("cand", None),
        P("cand", None),
        P("cand", None),
    )
    out_specs = (P(("src", "cand"), None, None), P(("src", "cand"), None), P(("src", "cand")))
    return jax.shard_map(
        functools.partial(shards, dict(mesh.shape)),
        mesh=mesh,
        in_specs=in_specs,
        out_specs=out_specs,
        check_vma=False,
    )
```

profile of v0, /device:TPU:0, one launch (start us, length us, event | category | flops | bytes accessed | tf_op | source)
XLA Modules:
  0.0 43.4 jit_solution(624862912436038984)
XLA Ops:
  1.3 39.7 %shard_map.103 = (bf16[128,1024]{1,0:T(8,128)(2,1)S(1)}, f32[1,4]{1,0:T(1,128)S(1)}, f32[1,1]{1,0:T(1,128)S(1)}) custom-call(bf16[128,1024]{1,0:T(8,128)(2,1)} %bitcast.4, s32[1,128]{1,0:T(1,128)} %ids_hbm.1, s32[1]{0:T(128)S(6)} %copy.17.used, f32[50265]{0:T(1024)} %table_hbm.1, bf16[256,1024]{1,0:T(8,128)(2,1)} %q_hbm.1, bf16[256,1024]{1,0:T(8,128)(2,1)} %k_hbm.1, ...), custom_call_target="tpu_custom_call" | custom-call | tf_op jit(solution)/shard_map/pallas_call | solution.py:409
  41.1 0.7 %copy.14 = bf16[1,128,1024]{2,1,0:T(8,128)(2,1)} copy(bf16[1,128,1024]{2,1,0:T(8,128)(2,1)S(1)} %bitcast.3) | data formatting | bytes 524288
  41.8 0.5 %copy.15 = f32[1,4]{1,0:T(1,128)} copy(f32[1,4]{1,0:T(1,128)S(1)} %get-tuple-element.10) | data formatting | bytes 32
where the time goes:
time: 43.6 us; the launch traced here: 43.4 us
  Pallas kernels  39.7 us (91%)
  between operations  2.45 us (6%)
  local copies, waits for them, and re-layouts  1.22 us (3%)
    pallas_call x1, Pallas kernels, shards(): pl.pallas_call(functools.partial(kernel, count), out_shape=(pltpu.VMEM((l...  39.7 us
    unnamed x2, local copies, waits for them, and re-layouts  1.22 us

commit v1 on v0

--- a/solution.py
+++ b/solution.py
@@ -143,9 +143,8 @@
     out_full,
     x_all,
     meta,
-    context_out,
-    context_full,
-    vectors,
+    context,
+    total,
     ids,
     table,
     local_sem,
@@ -160,7 +159,7 @@
     peer = [(group, flipped(me, bits)) for bits in range(count)]
     length, width = x_hbm.shape
     rows, columns = stage.shape[1], full.shape[2]
-    quarter, middle = rows // 4, length // 2
+    quarter = rows // 4
     started = []
 
     def push(src_ref, dst_ref, device):
@@ -207,14 +206,12 @@
         pl.semaphore_signal(barrier, inc=1, device_id=target, device_id_type=pl.DeviceIdType.MESH)
     pl.semaphore_wait(barrier, len(targets))
 
-    def exchange(held):
-        part = [held.at[0, pl.ds(0, middle), :], held.at[0, pl.ds(middle, middle), :]]
-
-        def slot(r, which):
-            return held.at[r, pl.ds(which * middle, middle), :]
-
-        first = {1: push(part[0], slot(1, 0), peer[1]), 2: push(part[1], slot(2, 1), peer[2])}
-        second = {1: push(part[1], slot(1, 1), peer[1]), 2: push(part[0], slot(2, 0), peer[2])}
+    def exchange(slot):
+        first = {1: push(slot(0, 0), slot(1, 0), peer[1]), 2: push(slot(0, 1), slot(2, 1), peer[2])}
+        second = {
+            1: push(slot(0, 1), slot(1, 1), peer[1]),
+            2: push(slot(0, 0), slot(2, 0), peer[2]),
+        }
 
         def relay():
             first[1].wait_recv()
@@ -224,8 +221,8 @@
 
         return second, relay
 
-    for t in range(3):
-        loads[t].wait()
+    for load in loads[:3]:
+        load.wait()
     w_copies = {}
     for r in others:
         w_copies[r] = push(
@@ -235,11 +232,18 @@
         )
     for load in loads[3:6]:
         load.wait()
-    o_copies = {
-        r: push(out_full.at[row_share(me, share), :], out_full.at[row_share(me, share), :], peer[r])
-        for r in others
-    }
-    x_second, x_relay = exchange(x_all)
+    half = length // 2
+    x_second, x_relay = exchange(lambda r, which: x_all.at[r, pl.ds(which * half, half), :])
+
+    def out_part(r, which, part):
+        start = (flipped(me, r) * rows) + which * quarter + part * (quarter // 2)
+        return out_full.at[pl.ds(pl.multiple_of(start, quarter // 2), quarter // 2), :]
+
+    def out_push(r, part, device):
+        return push(out_part(r, share, part), out_part(r, share, part), device)
+
+    o_first = {1: out_push(0, 0, peer[1]), 2: out_push(0, 1, peer[2])}
+    o_second = {1: out_push(0, 1, peer[1]), 2: out_push(0, 0, peer[2])}
     for load in loads[6:]:
         load.wait()
 
@@ -254,27 +258,25 @@
     meta[0] = jnp.concatenate([weights_row, jnp.broadcast_to(valid_row, (7, length))], axis=0)
     m_copies = {r: push(meta.at[0], meta.at[r], peer[r]) for r in others}
 
-    def spread(copy, landed):
-        copy.wait_recv()
+    def full_share(r, which):
+        return full.at[:, row_share(peer[r][1], which), :]
+
+    def out_share(r, which):
+        return out_full.at[row_share(peer[r][1], which), :]
+
+    def spread(landed):
         return (push(landed, landed, mate), push(landed, landed, sibling))
 
     def hand_over(copy, landed):
         copy.wait_recv()
         return push(landed, landed, sibling)
 
-    def full_share(r, which):
-        return full.at[:, row_share(peer[r][1], which), :]
-
-    def out_share(r, which):
-        return out_full.at[row_share(peer[r][1], which), :]
-
-    w_spread = {r: spread(w_copies[r], full_share(r, share)) for r in others}
-    o_spread = {}
-    o_hand = {}
+    w_spread = {}
     for r in others:
-        o_spread[r] = spread(o_copies[r], out_share(r, share))
+        w_copies[r].wait_recv()
+        w_spread[r] = spread(full_share(r, share))
+    x_far = x_relay()
     w_hand = {r: hand_over(w_spread[r][0], full_share(r, mate_share)) for r in others}
-    x_far = x_relay()
     for r in others:
         w_spread[r][1].wait_recv()
         w_hand[r].wait_recv()
@@ -309,41 +311,90 @@
             pieces.append(jnp.where(lane < HEAD, summed[:length], summed[length:]))
         return jnp.concatenate(pieces, axis=1).astype(jnp.bfloat16)
 
-    context_full[:, column_block(me)] = context_of(0)
-    c_copies = []
-    for r in others:
+    def context_part(r, candidate, part):
+        return context.at[r, candidate, pl.ds(part * half, half), :]
+
+    def context_push(r, candidate, part, way):
+        return push(
+            context_part(r, candidate, part),
+            context_part(r ^ way, candidate ^ way, part),
+            peer[way],
+        )
+
+    c_first, c_second = {}, {}
+
+    def attend(r):
+        context[0, r] = context_of(r)
+        c_first[r] = {1: context_push(0, r, 0, 1), 2: context_push(0, r, 1, 2)}
+        c_second[r] = {1: context_push(0, r, 1, 1), 2: context_push(0, r, 0, 2)}
+
+    attend(0)
+    for r in (1, 2):
         m_copies[r].wait_recv()
-        for copy in ((x_second[r],) if r < 3 else x_far):
-            copy.wait_recv()
-        context_out[r] = context_of(r)
-        c_copies.append(push(context_out.at[r], context_full.at[:, column_block(me)], peer[r]))
-        if r == 2:
-            for q in others:
-                o_hand[q] = hand_over(o_spread[q][0], out_share(q, mate_share))
-    for r in others:
+        x_second[r].wait_recv()
+        attend(r)
+    o_first[1].wait_recv()
+    o_near = out_push(1, 0, peer[2])
+    o_first[2].wait_recv()
+    o_far = out_push(2, 1, peer[1])
+    o_spread = {}
+    for r in (1, 2):
+        o_second[r].wait_recv()
+        o_spread[r] = spread(out_share(r, share))
+    m_copies[3].wait_recv()
+    for copy in x_far:
+        copy.wait_recv()
+    attend(3)
+    for copy in (o_near, o_far):
+        copy.wait_recv()
+    o_spread[3] = spread(out_share(3, share))
+
+    c_near, c_far = {}, {}
+    for r in range(count):
+        c_first[r][1].wait_recv()
+        c_near[r ^ 1] = context_push(1, r ^ 1, 0, 2)
+        c_first[r][2].wait_recv()
+        c_far[r ^ 2] = context_push(2, r ^ 2, 1, 1)
+    o_hand = {r: hand_over(o_spread[r][0], out_share(r, mate_share)) for r in others}
+
+    def out_rows(r):
+        return out_full[row_block(peer[r][1]), :]
+
+    def product(r):
+        return jnp.dot(
+            context[r].reshape(count * length, columns),
+            out_rows(r),
+            preferred_element_type=jnp.float32,
+        ).reshape(count, length, width)
+
+    total[...] = product(0)
+    for r in (1, 2):
         o_spread[r][1].wait_recv()
         o_hand[r].wait_recv()
-    for copy in c_copies:
-        copy.wait_recv()
-
-    mixed = jnp.dot(context_full[...], out_full[...], preferred_element_type=jnp.float32)
-    mixed = mixed + x_all[0].astype(jnp.float32)
-    centred = mixed - jnp.mean(mixed, axis=-1, keepdims=True)
-    squares = jnp.sum(centred * centred, axis=-1, keepdims=True)
-    own = (centred / jnp.sqrt(squares + 0.001)).astype(jnp.bfloat16)
-    vectors[0] = own
-    e_second, e_relay = exchange(vectors)
-    embedded_ref[...] = own
+        for candidate in range(count):
+            c_second[candidate][r].wait_recv()
+        total[...] += product(r)
+    o_spread[3][1].wait_recv()
+    o_hand[3].wait_recv()
 
     own_weight = meta[0, 0:1, :]
     own_column = jnp.broadcast_to(own_weight, (length, length)).T
     own_total = jnp.sum(own_weight, axis=1, keepdims=True)
     slot = lax.broadcasted_iota(jnp.int32, utility_ref.shape, 1)
 
-    def pair_of(r):
+    def vectors_of(r):
+        mixed = total[r] + jnp.dot(
+            context[3, r], out_rows(3), preferred_element_type=jnp.float32
+        )
+        mixed = mixed + x_all[r].astype(jnp.float32)
+        centred = mixed - jnp.mean(mixed, axis=-1, keepdims=True)
+        squares = jnp.sum(centred * centred, axis=-1, keepdims=True)
+        return (centred / jnp.sqrt(squares + 0.001)).astype(jnp.bfloat16)
+
+    def pair_of(own, far, r):
         far_weight = meta[r, 0:1, :]
         similar = lax.dot_general(
-            own, vectors[r], (((1,), (1,)), ((), ())), preferred_element_type=jnp.float32
+            own, far, (((1,), (1,)), ((), ())), preferred_element_type=jnp.float32
         )
         best_far = jnp.max(jnp.where(far_weight > 0, similar, -4.0), axis=1, keepdims=True)
         best_own = jnp.max(jnp.where(own_column > 0, similar, -4.0), axis=0, keepdims=True)
@@ -353,18 +404,22 @@
         )
         return 0.5 * (forward + backward)
 
-    diagonal = pair_of(0)
-    e_far = e_relay()
-    utility = jnp.where(slot == me, diagonal, 0.0)
-    everything = diagonal
-    for r in others:
-        for copy in ((e_second[r],) if r < 3 else e_far):
-            copy.wait_recv()
-        pair = pair_of(r)
+    vectors = {}
+    for r in (3, 2, 1, 0):
+        c_near[r ^ 2].wait_recv()
+        c_far[r ^ 1].wait_recv()
+        vectors[r] = vectors_of(r)
+    own = vectors[0]
+    embedded_ref[...] = own
+    utility = jnp.zeros(utility_ref.shape, jnp.float32)
+    everything = jnp.zeros(expected_ref.shape, jnp.float32)
+    for r in range(count):
+        pair = pair_of(own, vectors[r], r)
         utility = jnp.where(slot == peer[r][1], pair, utility)
-        everything = everything + pair
+        if r:
+            everything = everything + pair
     utility_ref[...] = utility
-    expected_ref[...] = (everything - diagonal) / (count - 1)
+    expected_ref[...] = everything / (count - 1)
 
     for copy in started:
         copy.wait_send()
@@ -405,7 +460,7 @@
         )
     anywhere = pl.BlockSpec(memory_space=pl.ANY)
     in_vmem = pl.BlockSpec(memory_space=pltpu.VMEM)
-    copies = pltpu.SemaphoreType.DMA((42,))
+    copies = pltpu.SemaphoreType.DMA((72,))
     embedded, utility, expected = pl.pallas_call(
         functools.partial(kernel, count),
         out_shape=(
@@ -421,9 +476,8 @@
             pltpu.VMEM((rows * count, width), jnp.bfloat16),
             pltpu.VMEM((count, length, width), jnp.bfloat16),
             pltpu.VMEM((count, 8, length), jnp.float32),
-            pltpu.VMEM((count, length, columns), jnp.bfloat16),
-            pltpu.VMEM((length, width), jnp.bfloat16),
-            pltpu.VMEM((count, length, width), jnp.bfloat16),
+            pltpu.VMEM((count, count, length, columns), jnp.bfloat16),
+            pltpu.VMEM((count, length, width), jnp.float32),
             pltpu.SMEM((1, length), jnp.int32),
             pltpu.SMEM(idf_table.shape, jnp.float32),
             pltpu.SemaphoreType.DMA((10,)),

time: 43.6 us -> 40.3 us (0.924)
  Pallas kernels: 39.7 us -> 36.5 us
    pallas_call x1, Pallas kernels: 39.7 us -> 36.5 us  [shards(): pl.pallas_call(functools.partial(kernel, count), out_shape=(pltpu.VMEM((l...]
where the time goes in v1:
time: 40.3 us; the launch traced here: 40.1 us
  Pallas kernels  36.5 us (91%)
  between operations  2.45 us (6%)
  local copies, waits for them, and re-layouts  1.22 us (3%)
    pallas_call x1, Pallas kernels, shards(): pl.pallas_call(functools.partial(kernel, count), out_shape=(pltpu.VMEM((l...  36.5 us
    unnamed x2, local copies, waits for them, and re-layouts  1.22 us

profile of v1, /device:TPU:0, one launch (start us, length us, event | category | flops | bytes accessed | tf_op | source)
XLA Modules:
  0.0 40.1 jit_solution(8165109155401252910)
XLA Ops:
  1.3 36.5 %shard_map.103 = (bf16[128,1024]{1,0:T(8,128)(2,1)S(1)}, f32[1,4]{1,0:T(1,128)S(1)}, f32[1,1]{1,0:T(1,128)S(1)}) custom-call(bf16[128,1024]{1,0:T(8,128)(2,1)} %bitcast.4, s32[1,128]{1,0:T(1,128)} %ids_hbm.1, s32[1]{0:T(128)S(6)} %copy.17.used, f32[50265]{0:T(1024)} %table_hbm.1, bf16[256,1024]{1,0:T(8,128)(2,1)} %q_hbm.1, bf16[256,1024]{1,0:T(8,128)(2,1)} %k_hbm.1, ...), custom_call_target="tpu_custom_call" | custom-call | tf_op jit(solution)/shard_map/pallas_call | solution.py:464
  37.8 0.7 %copy.14 = bf16[1,128,1024]{2,1,0:T(8,128)(2,1)} copy(bf16[1,128,1024]{2,1,0:T(8,128)(2,1)S(1)} %bitcast.3) | data formatting | bytes 524288
  38.5 0.5 %copy.15 = f32[1,4]{1,0:T(1,128)} copy(f32[1,4]{1,0:T(1,128)S(1)} %get-tuple-element.10) | data formatting | bytes 32

commit v2 on v1

--- a/solution.py
+++ b/solution.py
@@ -9,6 +9,7 @@
 from jax.sharding import PartitionSpec as P
 
 HEAD = 64
+SLOTS = 40
 
 
 def block_utility(own_vectors, own_weight, far_vectors, far_weight):
@@ -129,7 +130,7 @@
     count,
     x_hbm,
     ids_hbm,
-    used,
+    used_hbm,
     table_hbm,
     q_hbm,
     k_hbm,
@@ -145,11 +146,14 @@
     meta,
     context,
     total,
+    drain,
     ids,
+    used,
     table,
     local_sem,
     send_sem,
     recv_sem,
+    ready_sem,
 ):
     group, me = lax.axis_index("src"), lax.axis_index("cand")
     share = lax.rem(group, 4)
@@ -159,15 +163,24 @@
     peer = [(group, flipped(me, bits)) for bits in range(count)]
     length, width = x_hbm.shape
     rows, columns = stage.shape[1], full.shape[2]
-    quarter = rows // 4
-    started = []
-
-    def push(src_ref, dst_ref, device):
-        number = len(started)
-        copy = remote(src_ref, dst_ref, send_sem.at[number], recv_sem.at[number], device)
-        copy.start()
-        started.append(copy)
-        return copy
+    quarter, half = rows // 4, length // 2
+    sent, slots = [], []
+
+    def signal(semaphore, device):
+        pl.semaphore_signal(
+            semaphore, inc=1, device_id=device, device_id_type=pl.DeviceIdType.MESH
+        )
+
+    def slot():
+        slots.append(len(slots))
+        return slots[-1]
+
+    def push(src_ref, dst_ref, device, number):
+        remote(src_ref, dst_ref, send_sem.at[0], recv_sem.at[number], device).start()
+        sent.append(math.prod(src_ref.shape) * src_ref.dtype.itemsize)
+
+    def landed(number, like):
+        pltpu.make_async_copy(like, like, recv_sem.at[number]).wait()
 
     def column_block(index):
         return pl.ds(pl.multiple_of(index * columns, columns), columns)
@@ -182,104 +195,129 @@
     mate_share = lax.rem(share + 2, 4)
 
     weights = (q_hbm, k_hbm, v_hbm)
-    loads = [pltpu.make_async_copy(w, stage.at[t], local_sem.at[t]) for t, w in enumerate(weights)]
-    loads += [
-        pltpu.make_async_copy(o_hbm, out_full.at[row_block(me), :], local_sem.at[3]),
-        pltpu.make_async_copy(x_hbm, x_all.at[0], local_sem.at[4]),
-        pltpu.make_async_copy(ids_hbm, ids, local_sem.at[5]),
+    own_rows = out_full.at[row_block(me), :]
+    own_block = full.at[:, row_block(me), :]
+    for t, w in enumerate(weights):
+        pltpu.make_async_copy(w, stage.at[t], local_sem.at[0]).start()
+    load_o = pltpu.make_async_copy(o_hbm, own_rows, local_sem.at[1])
+    load_x = pltpu.make_async_copy(x_hbm, x_all.at[0], local_sem.at[2])
+    small = [
+        pltpu.make_async_copy(used_hbm, used, local_sem.at[3]),
+        pltpu.make_async_copy(ids_hbm, ids, local_sem.at[4]),
+        pltpu.make_async_copy(table_hbm, table, local_sem.at[5]),
     ]
-    loads += [
+    load_o.start()
+    load_x.start()
+    for load in small:
+        load.start()
+    for t, w in enumerate(weights):
         pltpu.make_async_copy(
-            w.at[:, column_block(me)], full.at[t, row_block(me), :], local_sem.at[6 + t]
-        )
-        for t, w in enumerate(weights)
-    ]
-    loads += [
-        pltpu.make_async_copy(table_hbm, table, local_sem.at[9]),
-    ]
-    for load in loads:
-        load.start()
+            w.at[:, column_block(me)], full.at[t, row_block(me), :], local_sem.at[6]
+        ).start()
 
     barrier = pltpu.get_barrier_semaphore()
-    targets = [sibling, mate] + [peer[r] for r in others]
+    targets = [sibling, mate, peer[1], peer[2]]
     for target in targets:
-        pl.semaphore_signal(barrier, inc=1, device_id=target, device_id_type=pl.DeviceIdType.MESH)
+        signal(barrier, target)
     pl.semaphore_wait(barrier, len(targets))
-
-    def exchange(slot):
-        first = {1: push(slot(0, 0), slot(1, 0), peer[1]), 2: push(slot(0, 1), slot(2, 1), peer[2])}
-        second = {
-            1: push(slot(0, 1), slot(1, 1), peer[1]),
-            2: push(slot(0, 0), slot(2, 0), peer[2]),
-        }
-
-        def relay():
-            first[1].wait_recv()
-            near = push(slot(1, 0), slot(3, 0), peer[2])
-            first[2].wait_recv()
-            return (near, push(slot(2, 1), slot(3, 1), peer[1]))
-
-        return second, relay
-
-    for load in loads[:3]:
-        load.wait()
-    w_copies = {}
-    for r in others:
-        w_copies[r] = push(
+    signal(ready_sem, peer[1])
+
+    def full_share(r, which):
+        return full.at[:, row_share(peer[r][1], which), :]
+
+    def out_share(r, which):
+        return out_full.at[row_share(peer[r][1], which), :]
+
+    def out_part(r, part):
+        start = peer[r][1] * rows + share * quarter + part * (quarter // 2)
+        return out_full.at[pl.ds(pl.multiple_of(start, quarter // 2), quarter // 2), :]
+
+    def x_part(r, part):
+        return x_all.at[r, pl.ds(part * half, half), :]
+
+    w_slot = {r: slot() for r in others}
+
+    def send_weights(r):
+        push(
             stage.at[:, own_share, column_block(peer[r][1])],
-            full.at[:, row_share(me, share), :],
+            full_share(0, share),
             peer[r],
-        )
-    for load in loads[3:6]:
-        load.wait()
-    half = length // 2
-    x_second, x_relay = exchange(lambda r, which: x_all.at[r, pl.ds(which * half, half), :])
-
-    def out_part(r, which, part):
-        start = (flipped(me, r) * rows) + which * quarter + part * (quarter // 2)
-        return out_full.at[pl.ds(pl.multiple_of(start, quarter // 2), quarter // 2), :]
-
-    def out_push(r, part, device):
-        return push(out_part(r, share, part), out_part(r, share, part), device)
-
-    o_first = {1: out_push(0, 0, peer[1]), 2: out_push(0, 1, peer[2])}
-    o_second = {1: out_push(0, 1, peer[1]), 2: out_push(0, 0, peer[2])}
-    for load in loads[6:]:
-        load.wait()
+            w_slot[r],
+        )
+
+    pltpu.make_async_copy(stage, stage, local_sem.at[0]).wait()
+    send_weights(1)
+    send_weights(2)
+    pl.semaphore_wait(ready_sem, 1)
+    send_weights(3)
+    load_o.wait()
+    o_first, o_second = {1: slot(), 2: slot()}, {1: slot(), 2: slot()}
+    push(out_part(0, 0), out_part(0, 0), peer[1], o_first[1])
+    push(out_part(0, 1), out_part(0, 1), peer[2], o_first[2])
+    push(out_part(0, 1), out_part(0, 1), peer[1], o_second[1])
+    push(out_part(0, 0), out_part(0, 0), peer[2], o_second[2])
+    load_x.wait()
+    x_first, x_second = {1: slot(), 2: slot()}, {1: slot(), 2: slot()}
+    push(x_part(0, 0), x_part(1, 0), peer[1], x_first[1])
+    push(x_part(0, 1), x_part(2, 1), peer[2], x_first[2])
+    push(x_part(0, 1), x_part(1, 1), peer[1], x_second[1])
+    push(x_part(0, 0), x_part(2, 0), peer[2], x_second[2])
 
     position = lax.broadcasted_iota(jnp.int32, (1, length), 1)
 
     def look_up(at, weights_row):
         return jnp.where(position == at, table[ids[0, at]], weights_row)
 
+    for load in small:
+        load.wait()
     valid_row = (position < used[0]).astype(jnp.float32)
     weights_row = lax.fori_loop(0, length, look_up, jnp.zeros((1, length), jnp.float32), unroll=8)
     weights_row = (weights_row * valid_row).astype(jnp.bfloat16).astype(jnp.float32)
     meta[0] = jnp.concatenate([weights_row, jnp.broadcast_to(valid_row, (7, length))], axis=0)
-    m_copies = {r: push(meta.at[0], meta.at[r], peer[r]) for r in others}
-
-    def full_share(r, which):
-        return full.at[:, row_share(peer[r][1], which), :]
-
-    def out_share(r, which):
-        return out_full.at[row_share(peer[r][1], which), :]
-
-    def spread(landed):
-        return (push(landed, landed, mate), push(landed, landed, sibling))
-
-    def hand_over(copy, landed):
-        copy.wait_recv()
-        return push(landed, landed, sibling)
-
-    w_spread = {}
+    m_slot = slot()
     for r in others:
-        w_copies[r].wait_recv()
-        w_spread[r] = spread(full_share(r, share))
-    x_far = x_relay()
-    w_hand = {r: hand_over(w_spread[r][0], full_share(r, mate_share)) for r in others}
+        push(meta.at[0], meta.at[r], peer[r], m_slot)
+
+    w_mate, w_near = {r: slot() for r in others}, slot()
     for r in others:
-        w_spread[r][1].wait_recv()
-        w_hand[r].wait_recv()
+        landed(w_slot[r], full_share(r, share))
+        push(full_share(r, share), full_share(r, share), mate, w_mate[r])
+        push(full_share(r, share), full_share(r, share), sibling, w_near)
+
+    def hand_weights(r):
+        landed(w_mate[r], full_share(r, mate_share))
+        push(full_share(r, mate_share), full_share(r, mate_share), sibling, w_near)
+
+    o_far = slot()
+    landed(o_first[1], out_part(1, 0))
+    push(out_part(1, 0), out_part(1, 0), peer[2], o_far)
+    landed(o_first[2], out_part(2, 1))
+    push(out_part(2, 1), out_part(2, 1), peer[1], o_far)
+    hand_weights(1)
+
+    o_mate, o_near = {r: slot() for r in others}, {r: slot() for r in others}
+
+    def spread_out(r):
+        push(out_share(r, share), out_share(r, share), mate, o_mate[r])
+        push(out_share(r, share), out_share(r, share), sibling, o_near[r])
+
+    def hand_out(r):
+        landed(o_mate[r], out_share(r, mate_share))
+        push(out_share(r, mate_share), out_share(r, mate_share), sibling, o_near[r])
+
+    landed(o_second[1], out_part(1, 1))
+    spread_out(1)
+    landed(o_second[2], out_part(2, 0))
+    spread_out(2)
+    hand_weights(2)
+    x_far = slot()
+    landed(x_first[1], x_part(1, 0))
+    push(x_part(1, 0), x_part(3, 0), peer[2], x_far)
+    landed(x_first[2], x_part(2, 1))
+    push(x_part(2, 1), x_part(3, 1), peer[1], x_far)
+    hand_weights(3)
+    pltpu.make_async_copy(own_block, own_block, local_sem.at[6]).wait()
+    landed(w_near, full.at[:, pl.ds(0, 6 * quarter), :])
 
     lane = lax.broadcasted_iota(jnp.int32, (1, 2 * HEAD), 1)
     scale = 1.0 / math.sqrt(HEAD)
@@ -303,90 +341,85 @@
             )
             scores = jnp.where(valid, scores, -1000000000.0)
             expo = jnp.exp(scores - jnp.max(scores, axis=-1, keepdims=True))
-            total = jnp.sum(expo, axis=-1, keepdims=True)
+            whole = jnp.sum(expo, axis=-1, keepdims=True)
             summed = jnp.dot(
                 expo.astype(jnp.bfloat16), v_pair, preferred_element_type=jnp.float32
             )
-            summed = summed / total
+            summed = summed / whole
             pieces.append(jnp.where(lane < HEAD, summed[:length], summed[length:]))
         return jnp.concatenate(pieces, axis=1).astype(jnp.bfloat16)
 
     def context_part(r, candidate, part):
         return context.at[r, candidate, pl.ds(part * half, half), :]
 
-    def context_push(r, candidate, part, way):
-        return push(
+    def context_push(r, candidate, part, way, number):
+        push(
             context_part(r, candidate, part),
             context_part(r ^ way, candidate ^ way, part),
             peer[way],
-        )
-
-    c_first, c_second = {}, {}
+            number,
+        )
+
+    c_first = {(r, way): slot() for r in range(count) for way in (1, 2)}
+    c_second = {r: slot() for r in range(count)}
+    c_far = {r: slot() for r in range(count)}
+
+    def product(r, candidate):
+        return jnp.dot(
+            context[r, candidate],
+            out_full[row_block(peer[r][1]), :],
+            preferred_element_type=jnp.float32,
+        )
 
     def attend(r):
         context[0, r] = context_of(r)
-        c_first[r] = {1: context_push(0, r, 0, 1), 2: context_push(0, r, 1, 2)}
-        c_second[r] = {1: context_push(0, r, 1, 1), 2: context_push(0, r, 0, 2)}
+        context_push(0, r, 0, 1, c_first[r, 1])
+        context_push(0, r, 1, 2, c_first[r, 2])
+        context_push(0, r, 1, 1, c_second[r])
+        context_push(0, r, 0, 2, c_second[r])
+
+    def begin(r):
+        total[r] = product(0, r) + x_all[r].astype(jnp.float32)
 
     attend(0)
-    for r in (1, 2):
-        m_copies[r].wait_recv()
-        x_second[r].wait_recv()
-        attend(r)
-    o_first[1].wait_recv()
-    o_near = out_push(1, 0, peer[2])
-    o_first[2].wait_recv()
-    o_far = out_push(2, 1, peer[1])
-    o_spread = {}
-    for r in (1, 2):
-        o_second[r].wait_recv()
-        o_spread[r] = spread(out_share(r, share))
-    m_copies[3].wait_recv()
-    for copy in x_far:
-        copy.wait_recv()
+    begin(0)
+    landed(m_slot, meta.at[pl.ds(1, count - 1)])
+    landed(x_second[1], x_part(1, 1))
+    attend(1)
+    begin(1)
+    landed(x_second[2], x_part(2, 0))
+    attend(2)
+    landed(o_far, out_share(3, share))
+    spread_out(3)
+    begin(2)
+    hand_out(1)
+    hand_out(2)
+    landed(x_far, x_all.at[3])
     attend(3)
-    for copy in (o_near, o_far):
-        copy.wait_recv()
-    o_spread[3] = spread(out_share(3, share))
-
-    c_near, c_far = {}, {}
+    begin(3)
+
     for r in range(count):
-        c_first[r][1].wait_recv()
-        c_near[r ^ 1] = context_push(1, r ^ 1, 0, 2)
-        c_first[r][2].wait_recv()
-        c_far[r ^ 2] = context_push(2, r ^ 2, 1, 1)
-    o_hand = {r: hand_over(o_spread[r][0], out_share(r, mate_share)) for r in others}
-
-    def out_rows(r):
-        return out_full[row_block(peer[r][1]), :]
-
-    def product(r):
-        return jnp.dot(
-            context[r].reshape(count * length, columns),
-            out_rows(r),
-            preferred_element_type=jnp.float32,
-        ).reshape(count, length, width)
-
-    total[...] = product(0)
-    for r in (1, 2):
-        o_spread[r][1].wait_recv()
-        o_hand[r].wait_recv()
-        for candidate in range(count):
-            c_second[candidate][r].wait_recv()
-        total[...] += product(r)
-    o_spread[3][1].wait_recv()
-    o_hand[3].wait_recv()
+        landed(c_first[r, 1], context_part(1, r ^ 1, 0))
+        context_push(1, r ^ 1, 0, 2, c_far[r ^ 3])
+        landed(c_first[r, 2], context_part(2, r ^ 2, 1))
+        context_push(2, r ^ 2, 1, 1, c_far[r ^ 3])
+        if r == 0:
+            for way in (1, 2):
+                landed(o_near[way], out_full.at[pl.ds(0, 2 * quarter), :])
+        landed(c_second[r], context.at[0, r])
+        total[r ^ 1] += product(1, r ^ 1)
+        total[r ^ 2] += product(2, r ^ 2)
+        if r == 1:
+            hand_out(3)
+    landed(o_near[3], out_full.at[pl.ds(0, 2 * quarter), :])
 
     own_weight = meta[0, 0:1, :]
     own_column = jnp.broadcast_to(own_weight, (length, length)).T
     own_total = jnp.sum(own_weight, axis=1, keepdims=True)
-    slot = lax.broadcasted_iota(jnp.int32, utility_ref.shape, 1)
+    place = lax.broadcasted_iota(jnp.int32, utility_ref.shape, 1)
 
     def vectors_of(r):
-        mixed = total[r] + jnp.dot(
-            context[3, r], out_rows(3), preferred_element_type=jnp.float32
-        )
-        mixed = mixed + x_all[r].astype(jnp.float32)
+        mixed = total[r] + product(3, r)
         centred = mixed - jnp.mean(mixed, axis=-1, keepdims=True)
         squares = jnp.sum(centred * centred, axis=-1, keepdims=True)
         return (centred / jnp.sqrt(squares + 0.001)).astype(jnp.bfloat16)
@@ -406,23 +439,22 @@
 
     vectors = {}
     for r in (3, 2, 1, 0):
-        c_near[r ^ 2].wait_recv()
-        c_far[r ^ 1].wait_recv()
+        landed(c_far[r], context.at[3, r])
         vectors[r] = vectors_of(r)
     own = vectors[0]
     embedded_ref[...] = own
     utility = jnp.zeros(utility_ref.shape, jnp.float32)
-    everything = jnp.zeros(expected_ref.shape, jnp.float32)
+    everything = jnp.zeros((1, 1), jnp.float32)
     for r in range(count):
         pair = pair_of(own, vectors[r], r)
-        utility = jnp.where(slot == peer[r][1], pair, utility)
+        utility = jnp.where(place == peer[r][1], pair, utility)
         if r:
             everything = everything + pair
     utility_ref[...] = utility
-    expected_ref[...] = everything / (count - 1)
-
-    for copy in started:
-        copy.wait_send()
+    expected_ref[0] = everything[0, 0] / (count - 1)
+
+    assert len(slots) <= SLOTS and sum(sent) == math.prod(drain.shape) * 2
+    pltpu.make_async_copy(drain, drain, send_sem.at[0]).wait()
 
 
 def shards(
@@ -460,16 +492,18 @@
         )
     anywhere = pl.BlockSpec(memory_space=pl.ANY)
     in_vmem = pl.BlockSpec(memory_space=pltpu.VMEM)
-    copies = pltpu.SemaphoreType.DMA((72,))
+    in_smem = pl.BlockSpec(memory_space=pltpu.SMEM)
+    sent = 12 * 3 * (rows // 4) * columns + 12 * (rows // 4) * width
+    sent += 3 * length * width + 3 * 16 * length + 12 * length * columns
     embedded, utility, expected = pl.pallas_call(
         functools.partial(kernel, count),
         out_shape=(
             pltpu.VMEM((length, width), jnp.bfloat16),
             pltpu.VMEM((1, count), jnp.float32),
-            pltpu.VMEM((1, 1), jnp.float32),
+            pltpu.SMEM((1,), jnp.float32),
         ),
-        in_specs=[anywhere] * 2 + [pl.BlockSpec(memory_space=pltpu.SMEM)] + [anywhere] * 5,
-        out_specs=(in_vmem, in_vmem, in_vmem),
+        in_specs=[anywhere] * 8,
+        out_specs=(in_vmem, in_vmem, in_smem),
         scratch_shapes=[
             pltpu.VMEM((3, rows, width), jnp.bfloat16),
             pltpu.VMEM((3, rows * count, columns), jnp.bfloat16),
@@ -478,11 +512,14 @@
             pltpu.VMEM((count, 8, length), jnp.float32),
             pltpu.VMEM((count, count, length, columns), jnp.bfloat16),
             pltpu.VMEM((count, length, width), jnp.float32),
+            pltpu.VMEM((sent // 128, 128), jnp.bfloat16),
             pltpu.SMEM((1, length), jnp.int32),
+            pltpu.SMEM((1,), jnp.int32),
             pltpu.SMEM(idf_table.shape, jnp.float32),
-            pltpu.SemaphoreType.DMA((10,)),
-            copies,
-            copies,
+            pltpu.SemaphoreType.DMA((7,)),
+            pltpu.SemaphoreType.DMA((1,)),
+            pltpu.SemaphoreType.DMA((SLOTS,)),
+            pltpu.SemaphoreType.REGULAR,
         ],
         compiler_params=pltpu.CompilerParams(collective_id=0, has_side_effects=True),
     )(
@@ -495,7 +532,7 @@
         value_weight,
         output_weight,
     )
-    return (embedded.reshape(1, length, width), utility, expected.reshape(1))
+    return (embedded.reshape(1, length, width), utility, expected)
 
 
 def solution(mesh):

time: 40.3 us -> 36 us (0.89)
  Pallas kernels: 36.5 us -> 32.8 us
  between operations: 2.45 us -> 1.81 us
    pallas_call x1, Pallas kernels: 36.5 us -> 32.8 us  [shards(): pl.pallas_call(functools.partial(kernel, count), out_shape=(pltpu.VMEM((l...]
where the time goes in v2:
time: 36 us; the launch traced here: 35.8 us
  Pallas kernels  32.8 us (91%)
  between operations  1.81 us (5%)
  local copies, waits for them, and re-layouts  1.22 us (3%)
    pallas_call x1, Pallas kernels, shards(): pl.pallas_call(functools.partial(kernel, count), out_shape=(pltpu.VMEM((l...  32.8 us
    unnamed x2, local copies, waits for them, and re-layouts  1.22 us

profile of v2, /device:TPU:0, one launch (start us, length us, event | category | flops | bytes accessed | tf_op | source)
XLA Modules:
  0.0 35.8 jit_solution(17398628127932481389)
XLA Ops:
  1.3 32.8 %shard_map.103 = (bf16[128,1024]{1,0:T(8,128)(2,1)S(1)}, f32[1,4]{1,0:T(1,128)S(1)}, f32[1]{0:T(128)S(4)}) custom-call(bf16[128,1024]{1,0:T(8,128)(2,1)} %bitcast.3, s32[1,128]{1,0:T(1,128)} %ids_hbm.1, s32[1]{0:T(128)S(6)} %copy.17.used_hbm, f32[50265]{0:T(1024)} %table_hbm.1, bf16[256,1024]{1,0:T(8,128)(2,1)} %q_hbm.1, bf16[256,1024]{1,0:T(8,128)(2,1)} %k_hbm.1, ...), custom_call_target="tpu_custom_call" | custom-call | tf_op jit(solution)/shard_map/pallas_call | solution.py:498
  34.6 0.7 %copy.14 = bf16[1,128,1024]{2,1,0:T(8,128)(2,1)} copy(bf16[1,128,1024]{2,1,0:T(8,128)(2,1)S(1)} %bitcast.2) | data formatting | bytes 524288
  35.3 0.5 %copy.15 = f32[1,4]{1,0:T(1,128)} copy(f32[1,4]{1,0:T(1,128)S(1)} %get-tuple-element.10) | data formatting | bytes 32

commit v3 on v2

--- a/solution.py
+++ b/solution.py
@@ -84,7 +84,7 @@
     centred = mixed - jnp.mean(mixed, axis=-1, keepdims=True)
     squares = jnp.sum(centred * centred, axis=-1, keepdims=True)
     embedded = (
-        (centred / jnp.sqrt(squares + 0.001))
+        (centred * (1.0 / jnp.sqrt(squares + 0.001)))
         .astype(jnp.bfloat16)
         .reshape(local_cands, length, width)
     )
@@ -413,45 +413,41 @@
             hand_out(3)
     landed(o_near[3], out_full.at[pl.ds(0, 2 * quarter), :])
 
-    own_weight = meta[0, 0:1, :]
-    own_column = jnp.broadcast_to(own_weight, (length, length)).T
-    own_total = jnp.sum(own_weight, axis=1, keepdims=True)
+    weight_of = [meta[r, 0:1, :] for r in range(count)]
+    sum_of = [jnp.sum(weights_row, axis=1, keepdims=True) for weights_row in weight_of]
+    own_column = jnp.broadcast_to(weight_of[0], (length, length)).T
+    own_usable = own_column > 0
+    column = own_column[:, 0:1]
     place = lax.broadcasted_iota(jnp.int32, utility_ref.shape, 1)
 
     def vectors_of(r):
         mixed = total[r] + product(3, r)
         centred = mixed - jnp.mean(mixed, axis=-1, keepdims=True)
         squares = jnp.sum(centred * centred, axis=-1, keepdims=True)
-        return (centred / jnp.sqrt(squares + 0.001)).astype(jnp.bfloat16)
+        return (centred * (1.0 / jnp.sqrt(squares + 0.001))).astype(jnp.bfloat16)
 
     def pair_of(own, far, r):
-        far_weight = meta[r, 0:1, :]
         similar = lax.dot_general(
             own, far, (((1,), (1,)), ((), ())), preferred_element_type=jnp.float32
         )
-        best_far = jnp.max(jnp.where(far_weight > 0, similar, -4.0), axis=1, keepdims=True)
-        best_own = jnp.max(jnp.where(own_column > 0, similar, -4.0), axis=0, keepdims=True)
-        forward = jnp.sum(own_column[:, 0:1] * best_far, axis=0, keepdims=True) / own_total
-        backward = jnp.sum(far_weight * best_own, axis=1, keepdims=True) / jnp.sum(
-            far_weight, axis=1, keepdims=True
-        )
+        best_far = jnp.max(jnp.where(weight_of[r] > 0, similar, -4.0), axis=1, keepdims=True)
+        best_own = jnp.max(jnp.where(own_usable, similar, -4.0), axis=0, keepdims=True)
+        forward = jnp.sum(column * best_far, axis=0, keepdims=True) / sum_of[0]
+        backward = jnp.sum(weight_of[r] * best_own, axis=1, keepdims=True) / sum_of[r]
         return 0.5 * (forward + backward)
 
     vectors = {}
     for r in (3, 2, 1, 0):
         landed(c_far[r], context.at[3, r])
         vectors[r] = vectors_of(r)
-    own = vectors[0]
-    embedded_ref[...] = own
+        if r == 0:
+            embedded_ref[...] = vectors[0]
+    pair = [pair_of(vectors[0], vectors[r], r) for r in range(count)]
     utility = jnp.zeros(utility_ref.shape, jnp.float32)
-    everything = jnp.zeros((1, 1), jnp.float32)
     for r in range(count):
-        pair = pair_of(own, vectors[r], r)
-        utility = jnp.where(place == peer[r][1], pair, utility)
-        if r:
-            everything = everything + pair
+        utility = jnp.where(place == peer[r][1], pair[r], utility)
     utility_ref[...] = utility
-    expected_ref[0] = everything[0, 0] / (count - 1)
+    expected_ref[0] = (pair[1] + pair[2] + pair[3])[0, 0] / (count - 1)
 
     assert len(slots) <= SLOTS and sum(sent) == math.prod(drain.shape) * 2
     pltpu.make_async_copy(drain, drain, send_sem.at[0]).wait()

time: 36 us -> 36 us (level)
  no operation moved by 1% of the time
where the time goes in v3:
time: 36 us; the launch traced here: 35.8 us
  Pallas kernels  32.8 us (91%)
  between operations  1.81 us (5%)
  local copies, waits for them, and re-layouts  1.22 us (3%)
    pallas_call x1, Pallas kernels, shards(): pl.pallas_call(functools.partial(kernel, count), out_shape=(pltpu.VMEM((l...  32.8 us
    unnamed x2, local copies, waits for them, and re-layouts  1.22 us

profile of v3, /device:TPU:0, one launch (start us, length us, event | category | flops | bytes accessed | tf_op | source)
XLA Modules:
  0.0 35.8 jit_solution(4515331307657486542)
XLA Ops:
  1.3 32.8 %shard_map.103 = (bf16[128,1024]{1,0:T(8,128)(2,1)S(1)}, f32[1,4]{1,0:T(1,128)S(1)}, f32[1]{0:T(128)S(4)}) custom-call(bf16[128,1024]{1,0:T(8,128)(2,1)} %bitcast.3, s32[1,128]{1,0:T(1,128)} %ids_hbm.1, s32[1]{0:T(128)S(6)} %copy.17.used_hbm, f32[50265]{0:T(1024)} %table_hbm.1, bf16[256,1024]{1,0:T(8,128)(2,1)} %q_hbm.1, bf16[256,1024]{1,0:T(8,128)(2,1)} %k_hbm.1, ...), custom_call_target="tpu_custom_call" | custom-call | tf_op jit(solution)/shard_map/pallas_call | solution.py:494
  34.6 0.7 %copy.14 = bf16[1,128,1024]{2,1,0:T(8,128)(2,1)} copy(bf16[1,128,1024]{2,1,0:T(8,128)(2,1)S(1)} %bitcast.2) | data formatting | bytes 524288
  35.3 0.5 %copy.15 = f32[1,4]{1,0:T(1,128)} copy(f32[1,4]{1,0:T(1,128)S(1)} %get-tuple-element.10) | data formatting | bytes 32
